TPU v7x, 32 devices: a whole 2x2x4 slice. The times are simulated.
32 devices in a mesh: sample: 8 (over y, x, core), line: 4 (over z).
Axes of the slice: x: 2, y: 2, z: 4, core: 2. Of those that a mesh axis runs over, the one named last changes fastest.
Arguments:
- wind_dev: bfloat16 [4096, 10000], P('sample', 'line'), may hold values from -6 to 6
- ptdf: bfloat16 [4096, 10000], P('line'), may hold values from -0.0625 to 0.0625
- region_weights: bfloat16 [31, 10000], replicated, may hold values from -0.0625 to 0.0625
- incidence: int32 [12706, 2], replicated, may hold values from 0 to 9999
- monitored: int32 [4096], P('line'), may hold values from 0 to 12705
- ratings: float32 [12706], replicated, may hold values from 1 to 3
- base_flow: float32 [4096], P('line'), may hold values from -6 to 6
- line_cost: float32 [4096], P('line'), may hold values from 0.2 to 20
- policy: float32 [32, 4096], P(None, 'line'), may hold values from -0.6 to 0.6
Outputs:
- new_policy: float32 [32, 4096], P(None, 'line')
- new_flows: float32 [4096, 4096], P('sample', 'line')
- decrement: float32 [], replicated
- grad_norm: float32 [], replicated
All inputs are finite; a program needn't handle non-finite values.
Results may differ from a plain program's by a relative error of at most 0.0003.
Values may be sent and summed in bfloat16 or wider, within the bound.
A program may use at most 128 MiB of HBM per device.

v0:
```python
import jax
import jax.numpy as jnp
from jax import lax
from jax.experimental import pallas as pl
from jax.experimental.pallas import tpu as pltpu
from jax.sharding import PartitionSpec as P

ridge_weight = 1.0
barrier_weight = 0.1
smoothing = 0.5


def solve_lines(regions, packed_ref, weight_ref, policy_ref, out_ref, cols_ref):
    features = regions + 1
    weight = weight_ref[...]
    policy = policy_ref[...]
    margin_sq = 1.0 - policy * policy
    diag_terms = ridge_weight + barrier_weight * 2.0 * (1.0 + policy * policy) / (
        margin_sq * margin_sq
    )
    cols_ref[...] = jnp.zeros_like(cols_ref)
    bands = (regions + 1) // 2
    for band in range(bands):
        rows = packed_ref[band * features : (band + 1) * features, :] * weight
        if band == 0:
            rows = rows + diag_terms
        for i in range(regions):
            j = (i + band) % regions
            cols_ref[min(i, j), max(i, j) : max(i, j) + 1, :] = rows[i : i + 1]
    cross = packed_ref[bands * features : (bands + 1) * features, :] * weight
    for i in range(regions):
        cols_ref[i, regions : regions + 1, :] = cross[i : i + 1]
    cols_ref[regions, regions : regions + 1, :] = cross[regions:] + diag_terms[regions:]
    gradient = packed_ref[(bands + 1) * features : (bands + 2) * features, :] * weight
    gradient = gradient + ridge_weight * policy + barrier_weight * 2.0 * policy / margin_sq
    grad_sq = jnp.sum(gradient * gradient, axis=0, keepdims=True)

    positions = lax.broadcasted_iota(jnp.int32, gradient.shape, 0)
    inverses, forward = [], []
    running = gradient
    forward_sq = jnp.zeros_like(weight)
    for k in range(features):
        column = cols_ref[k]
        inverse = 1.0 / jnp.sqrt(column[k : k + 1])
        column = jnp.where(positions >= k, column * inverse, 0.0)
        cols_ref[k] = column
        value = running[k : k + 1] * inverse
        running = running - column * value
        forward_sq = forward_sq + value * value
        inverses.append(inverse)
        forward.append(value)
        for j in range(k + 1, features):
            base = j // 8 * 8
            cols_ref[j, base:, :] = cols_ref[j, base:, :] - column[base:] * column[j : j + 1]
    solved = jnp.zeros_like(gradient)
    for k in reversed(range(features)):
        value = (
            forward[k] - jnp.sum(cols_ref[k] * solved, axis=0, keepdims=True)
        ) * inverses[k]
        solved = jnp.where(positions == k, value, solved)
    out_ref[...] = jnp.zeros_like(out_ref)
    out_ref[:features, :] = -solved
    out_ref[features : features + 1, :] = forward_sq
    out_ref[features + 1 : features + 2, :] = grad_sq


def greet(partners):
    barrier = pltpu.get_barrier_semaphore()
    for partner in partners:
        pl.semaphore_signal(
            barrier, inc=1, device_id=partner, device_id_type=pl.DeviceIdType.MESH
        )
    pl.semaphore_wait(barrier, len(partners))


def share_steps(samples, ring, features, solved_ref, all_ref, sums_ref, got_ref, mine_ref, far_ref, sends, recvs):
    me, place = lax.axis_index("sample"), lax.axis_index("line")
    peers = [lax.rem(me + i, samples) for i in range(1, samples)]
    lines = [lax.rem(place + i, ring) for i in range(1, ring)]
    copies = []
    for slot, peer in enumerate(peers):
        copies.append(
            pltpu.make_async_remote_copy(
                src_ref=solved_ref,
                dst_ref=got_ref.at[slot],
                send_sem=sends.at[slot],
                recv_sem=recvs.at[slot],
                device_id={"sample": peer},
                device_id_type=pl.DeviceIdType.MESH,
            )
        )
        copies[-1].start()
    total = solved_ref[features:, :]
    for slot in range(samples - 1):
        copies[slot].wait_recv()
        total = total + got_ref[slot, features:, :]
    mine_ref[...] = total
    all_ref[me] = solved_ref[:features, :]
    for slot in range(samples - 1):
        source = lax.rem(me + samples - 1 - slot, samples)
        all_ref[source] = got_ref[slot, :features, :]
    far = []
    for slot, line in enumerate(lines):
        far.append(
            pltpu.make_async_remote_copy(
                src_ref=mine_ref,
                dst_ref=far_ref.at[slot],
                send_sem=sends.at[samples - 1 + slot],
                recv_sem=recvs.at[samples - 1 + slot],
                device_id={"line": line},
                device_id_type=pl.DeviceIdType.MESH,
            )
        )
        far[-1].start()
    total = mine_ref[...]
    for slot in range(ring - 1):
        far[slot].wait_recv()
        total = total + far_ref[slot]
    sums_ref[...] = total
    for copy in copies + far:
        copy.wait_send()


def split(value):
    top = value.astype(jnp.bfloat16)
    return top, (value - top.astype(jnp.float32)).astype(jnp.bfloat16)


def dot3(left, right):
    left_top, left_rest = split(left)
    right_top, right_rest = split(right)

    def product(a, b):
        return lax.dot_general(a, b, (((1,), (0,)), ((), ())), preferred_element_type=jnp.float32)

    return product(left_top, right_top) + (
        product(left_top, right_rest) + product(left_rest, right_top)
    )


def split_rows(width, total, ring):
    rows = (width + 15 + 15) // 16 * 16
    starts = [min(piece * width // 16 * 16, total - rows) for piece in range(ring)]
    return rows, starts


def newton_kernel(
    samples, ring, chunk, block, group,
    wind_ref, ptdf_ref, weights_ref, ends_ref, ratings_ref, monitored_ref, base_ref, cost_ref,
    policy_ref,
    policy_out, flow_out, size_out,
    diff_ref, factors_ref, all_ref, sums_ref, winds, grids, region_mix, stage, table, found, spread, outbox, inbox, mix_inbox,
    packed, weight_mine, policy_mine, cols, solved, step_inbox, mine, far,
    own_sem, stage_sems, send_up, recv_up, send_down, recv_down,
    send_out, recv_out, send_mix, recv_mix, send_step, recv_step,
):
    me, mine_s = lax.axis_index("line"), lax.axis_index("sample")
    regions = weights_ref.shape[0]
    features = regions + 1
    width, scen_here = wind_ref.shape
    total, lines_here = ptdf_ref.shape
    grid_lines = ends_ref.shape[1]
    share = lines_here // samples
    chunks = scen_here // chunk
    blocks = lines_here // block
    bands = (regions + 1) // 2
    reach = ring - 1
    f32, bf16 = jnp.float32, jnp.bfloat16
    peers = [lax.rem(mine_s + i, samples) for i in range(1, samples)]
    greet(
        [{"line": lax.rem(me + i, ring)} for i in range(1, ring)]
        + [{"sample": peer} for peer in peers]
    )

    def rows_of(step):
        return pl.ds(pl.multiple_of(step * chunk, chunk), chunk)

    def transfer(step, hops, side):
        piece = me - side * (hops - 1)
        slot = step * reach + hops - 1
        rows = rows_of(step)
        first = isinstance(hops, int) and hops == 1
        source = wind_ref.at[:, rows] if first else winds.at[piece, :, rows]
        sends_, recvs = (send_up, recv_up) if side == 1 else (send_down, recv_down)
        return pltpu.make_async_remote_copy(
            src_ref=source,
            dst_ref=winds.at[piece, :, rows],
            send_sem=sends_.at[slot],
            recv_sem=recvs.at[slot],
            device_id={"line": me + side},
            device_id_type=pl.DeviceIdType.MESH,
        )

    def transfer_first(step):
        for side in (1, -1):
            @pl.when(sends(1, side))
            def _():
                transfer(step, 1, side).wait_send()

    def sends(hops, side):
        if side == 1:
            return jnp.logical_and(me >= hops - 1, me < ring - 1)
        return jnp.logical_and(me <= ring - hops, me > 0)

    def receives(hops, side):
        return me >= hops if side == 1 else me < ring - hops

    def launch(step, hops):
        for side in (1, -1):
            @pl.when(sends(hops, side))
            def _():
                transfer(step, hops, side).start()

    def arrival(step, hops, side):
        slot = step * reach + hops - 1
        here = winds.at[me - side * hops, :, rows_of(step)]
        pltpu.make_async_remote_copy(
            src_ref=here,
            dst_ref=here,
            send_sem=(send_up if side == 1 else send_down).at[slot],
            recv_sem=(recv_up if side == 1 else recv_down).at[slot],
            device_id={"line": me - side},
            device_id_type=pl.DeviceIdType.MESH,
        ).wait_recv()

    launch(0, 1)
    if chunks > 1:
        launch(1, 1)
    own = pltpu.make_async_copy(wind_ref, winds.at[me], own_sem)
    own.start()

    stage_rows, starts = split_rows(width, total, ring)

    def staged(piece, index):
        slot = lax.rem(index, 2)
        return pltpu.make_async_copy(
            ptdf_ref.at[
                pl.ds(starts[piece], stage_rows), pl.ds(pl.multiple_of(index * block, block), block)
            ],
            stage.at[slot],
            stage_sems.at[slot],
        )

    region_mix[...] = jnp.zeros_like(region_mix)
    for piece in range(ring):
        region_mix[piece, :regions, :] = weights_ref[:, width * piece : width * (piece + 1)]
        skip = width * piece - starts[piece]
        staged(piece, 0).start()

        def place(index, carry):
            @pl.when(index + 1 < blocks)
            def _():
                staged(piece, index + 1).start()

            staged(piece, index).wait()
            lines = pl.ds(pl.multiple_of(index * block, block), block)
            grids[piece, :, lines] = stage[lax.rem(index, 2), skip : skip + width, :]
            return carry

        lax.fori_loop(0, blocks, place, 0)

    ends = ends_ref[...]
    rating_all = ratings_ref[...]
    first = rating_all.astype(bf16).astype(f32)
    second = (rating_all - first).astype(bf16).astype(f32)
    third = rating_all - first - second
    table[...] = jnp.zeros_like(table)
    table[:, :grid_lines] = jnp.concatenate(
        [
            (ends // 256).astype(f32),
            lax.rem(ends, 256).astype(f32),
            first,
            second,
            third,
            jnp.zeros_like(first),
        ],
        axis=0,
    ).astype(bf16)
    found[...] = jnp.zeros_like(found)

    def lookup(index, carry):
        where = pl.ds(pl.multiple_of(index * group, group), group)
        hot = (
            lax.broadcasted_iota(jnp.int32, (group, lines_here), 0) + index * group
            == monitored_ref[...]
        )
        found[...] += lax.dot_general(
            table[:, where],
            jnp.where(hot, 1.0, 0.0).astype(bf16),
            (((1,), (0,)), ((), ())),
            preferred_element_type=f32,
        )
        return carry

    lax.fori_loop(0, table.shape[1] // group, lookup, 0)
    from_bus = found[0:1, :] * 256.0 + found[2:3, :]
    to_bus = found[1:2, :] * 256.0 + found[3:4, :]
    rating_row = found[4:5, :] + found[5:6, :] + found[6:7, :]
    found[0:1, :] = from_bus
    found[1:2, :] = to_bus
    for d in range(samples):
        cut = slice(d * share, (d + 1) * share)
        spread[d, :features, :] = policy_ref[:, cut]
        spread[d, features : features + 1, :] = cost_ref[:, cut]
        spread[d, features + 1 : features + 2, :] = rating_row[:, cut]
    policy_mine[...] = spread[mine_s, :features, :]
    weight_mine[...] = spread[mine_s, features : features + 1, :] / (scen_here * samples)
    packed[...] = jnp.zeros_like(packed)
    own.wait()

    forward = (((1,), (0,)), ((), ()))

    def add_piece(step, piece):
        rows = rows_of(step)
        wind = winds[piece, :, rows]
        turned = wind.T
        buses = (
            lax.broadcasted_iota(jnp.int32, (width, block), 0) + piece * width
        ).astype(f32)

        def one(index, carry):
            lines = pl.ds(pl.multiple_of(index * block, block), block)
            pick = jnp.where(buses == found[1:2, lines], 1.0, 0.0) - jnp.where(
                buses == found[0:1, lines], 1.0, 0.0
            )
            grid = lax.dot_general(
                turned, grids[piece, :, lines], forward, preferred_element_type=f32
            )
            diff = lax.dot_general(
                turned, pick.astype(bf16), forward, preferred_element_type=f32
            )
            flow_out[rows, lines] += grid
            diff_ref[rows, lines] += diff
            return carry

        lax.fori_loop(0, blocks, one, 0)
        mix = lax.dot_general(region_mix[piece], wind, forward, preferred_element_type=f32)
        factors_ref[:, rows] += mix

    def finish(step):
        rows = rows_of(step)
        turned = factors_ref[:, rows].T
        mix_inbox[mine_s, step] = factors_ref[:, rows]
        diff = diff_ref[rows, :]
        flow = (
            flow_out[rows, :]
            + base_ref[...]
            + dot3(turned, policy_ref[...])
            + policy_ref[regions:, :] * diff
        )
        flow_out[rows, :] = flow
        for d in range(samples):
            cut = slice(d * share, (d + 1) * share)
            outbox[d, step, 0] = flow[:, cut].astype(bf16)
            outbox[d, step, 1] = diff[:, cut].astype(bf16)

    def parcel(step, slot, peer, source):
        spot = step * (samples - 1) + slot
        common = dict(device_id={"sample": peer}, device_id_type=pl.DeviceIdType.MESH)
        return (
            pltpu.make_async_remote_copy(
                src_ref=outbox.at[peer, step],
                dst_ref=inbox.at[source, step],
                send_sem=send_out.at[spot],
                recv_sem=recv_out.at[spot],
                **common,
            ),
            pltpu.make_async_remote_copy(
                src_ref=mix_inbox.at[mine_s, step],
                dst_ref=mix_inbox.at[source, step],
                send_sem=send_mix.at[spot],
                recv_sem=recv_mix.at[spot],
                **common,
            ),
        )

    def deliver(step):
        for slot, peer in enumerate(peers):
            for copy in parcel(step, slot, peer, mine_s):
                copy.start()

    def collect(step):
        inbox[mine_s, step] = outbox[mine_s, step]
        rating = spread[mine_s, features + 1 : features + 2, :]

        def one(turn, carry):
            source = lax.rem(mine_s + samples - turn, samples)

            @pl.when(turn > 0)
            def _():
                for copy in parcel(step, turn - 1, source, source):
                    copy.wait_recv()

            flow = inbox[source, step, 0].astype(f32)
            diff = inbox[source, step, 1].astype(f32)
            factors = mix_inbox[source, step]
            doubled = jnp.concatenate(
                [factors[:regions], factors[:regions], factors[regions:]], axis=0
            )
            pairs = jnp.concatenate(
                [doubled[d : d + features] * factors for d in range(bands)], axis=0
            )
            prob_up = jax.nn.sigmoid((flow - rating) / smoothing)
            prob_down = jax.nn.sigmoid((-flow - rating) / smoothing)
            slope = prob_up - prob_down
            curve = (prob_up * (1.0 - prob_up) + prob_down * (1.0 - prob_down)) / smoothing
            weighted = curve * diff
            top = bands * features
            packed[:top, :] += dot3(pairs, curve)
            packed[top : top + regions, :] += dot3(factors, weighted)[:regions]
            packed[top + regions : top + features, :] += jnp.sum(
                weighted * diff, axis=0, keepdims=True
            )
            low = top + features
            packed[low : low + regions, :] += dot3(factors, slope)[:regions]
            packed[low + regions : low + features, :] += jnp.sum(
                slope * diff, axis=0, keepdims=True
            )
            return carry

        lax.fori_loop(0, samples, one, 0)

    flow_out[...] = jnp.zeros_like(flow_out)
    diff_ref[...] = jnp.zeros_like(diff_ref)
    factors_ref[...] = jnp.zeros_like(factors_ref)

    def advance(step, carry):
        @pl.when(step + 2 < chunks)
        def _():
            launch(step + 2, 1)

        def visit(turn, inner):
            hops = (turn + 1) // 2

            @pl.when(lax.rem(turn, 2) == 1)
            def _():
                for side in (1, -1):
                    @pl.when(receives(hops, side))
                    def _():
                        arrival(step, hops, side)

                @pl.when(hops < reach)
                def _():
                    launch(step, hops + 1)

            piece = me + hops * (1 - 2 * lax.rem(turn, 2))

            @pl.when(jnp.logical_and(piece >= 0, piece < ring))
            def _():
                add_piece(step, piece)

            return inner

        lax.fori_loop(0, 2 * ring - 1, visit, 0)
        finish(step)
        deliver(step)

        @pl.when(step > 0)
        def _():
            collect(step - 1)

        return carry

    lax.fori_loop(0, chunks, advance, 0)
    collect(chunks - 1)
    solve_lines(regions, packed, weight_mine, policy_mine, solved, cols)
    share_steps(
        samples, ring, features, solved, all_ref, sums_ref, step_inbox, mine, far,
        send_step, recv_step,
    )
    sizes = jnp.sqrt(jnp.sum(sums_ref[...], axis=1, keepdims=True))
    size_out[...] = sizes[:2]
    scale = 1.0 / (
        1.0 + sizes[:1] / ((barrier_weight * features * lines_here * ring) ** 0.5)
    )
    scaled = scale * jnp.concatenate([all_ref[d] for d in range(samples)], axis=1)
    policy_out[...] = policy_ref[...] + scaled

    def update(step, carry):
        rows = rows_of(step)
        turned = factors_ref[:, rows].T
        flow_out[rows, :] += dot3(turned, scaled) + scaled[regions:, :] * diff_ref[rows, :]
        return carry

    lax.fori_loop(0, chunks, update, 0)

    def drain(step, carry):
        def line_drain(hops, inner):
            for side in (1, -1):
                @pl.when(sends(hops, side))
                def _():
                    transfer(step, hops, side).wait_send()
            return inner

        transfer_first(step)
        lax.fori_loop(2, ring, line_drain, 0)
        for slot, peer in enumerate(peers):
            for copy in parcel(step, slot, peer, mine_s):
                copy.wait_send()
        return carry

    lax.fori_loop(0, chunks, drain, 0)


def newton_steps(
    wind_dev, ptdf, region_weights, incidence, monitored, ratings, base_flow, line_cost, policy
):
    samples, ring = lax.axis_size("sample"), lax.axis_size("line")
    scen_here, width = wind_dev.shape
    lines_here, total = ptdf.shape
    features = policy.shape[0]
    share = lines_here // samples
    chunk = 128
    chunks = scen_here // chunk
    block = 256
    while lines_here % block:
        block //= 2
    group = 512
    table_cols = (incidence.shape[0] + group - 1) // group * group
    stage_rows, _ = split_rows(width, total, ring)
    packed_rows = (features // 2 + 2) * features
    hops = chunks * (ring - 1)
    parcels = chunks * (samples - 1)
    copies = samples + ring - 2
    vmem = pl.BlockSpec(memory_space=pltpu.VMEM)
    anywhere = pl.BlockSpec(memory_space=pl.ANY)
    f32, bf16 = jnp.float32, jnp.bfloat16
    dma = pltpu.SemaphoreType.DMA
    return pl.pallas_call(
        lambda *refs: newton_kernel(samples, ring, chunk, block, group, *refs),
        out_shape=(
            jax.ShapeDtypeStruct((features, lines_here), f32),
            jax.ShapeDtypeStruct((scen_here, lines_here), f32),
            jax.ShapeDtypeStruct((2, 1), f32),
        ),
        in_specs=[anywhere, anywhere] + [vmem] * 7,
        out_specs=(vmem,) * 3,
        scratch_shapes=[
            pltpu.VMEM((scen_here, lines_here), f32),
            pltpu.VMEM((features, scen_here), f32),
            pltpu.VMEM((samples, features, share), f32),
            pltpu.VMEM((8, share), f32),
            pltpu.VMEM((ring, width, scen_here), bf16),
            pltpu.VMEM((ring, width, lines_here), bf16),
            pltpu.VMEM((ring, features, width), bf16),
            pltpu.VMEM((2, stage_rows, block), bf16),
            pltpu.VMEM((8, table_cols), bf16),
            pltpu.VMEM((8, lines_here), f32),
            pltpu.VMEM((samples, features + 8, share), f32),
            pltpu.VMEM((samples, chunks, 2, chunk, share), bf16),
            pltpu.VMEM((samples, chunks, 2, chunk, share), bf16),
            pltpu.VMEM((samples, chunks, features, chunk), f32),
            pltpu.VMEM((packed_rows, share), f32),
            pltpu.VMEM((1, share), f32),
            pltpu.VMEM((features, share), f32),
            pltpu.VMEM((features, features, share), f32),
            pltpu.VMEM((features + 8, share), f32),
            pltpu.VMEM((samples - 1, features + 8, share), f32),
            pltpu.VMEM((8, share), f32),
            pltpu.VMEM((ring - 1, 8, share), f32),
            dma,
            dma((2,)),
            dma((hops,)),
            dma((hops,)),
            dma((hops,)),
            dma((hops,)),
            dma((parcels,)),
            dma((parcels,)),
            dma((parcels,)),
            dma((parcels,)),
            dma((copies,)),
            dma((copies,)),
        ],
        compiler_params=pltpu.CompilerParams(
            collective_id=0, has_side_effects=True, vmem_limit_bytes=67000000
        ),
        name="newton_steps",
    )(
        wind_dev.T, ptdf.T, region_weights, incidence.T, ratings[None, :], monitored[None, :],
        base_flow[None, :], line_cost[None, :], policy,
    )


def shards(*arrays):
    new_policy, new_flows, sizes = newton_steps(*arrays)
    return new_policy, new_flows, sizes[0, 0], sizes[1, 0]


def solution(mesh):
    placed = (
        P("sample", "line"),
        P("line", None),
        P(),
        P(),
        P("line"),
        P(),
        P("line"),
        P("line"),
        P(None, "line"),
    )
    return jax.shard_map(
        shards,
        mesh=mesh,
        in_specs=placed,
        out_specs=(P(None, "line"), P("sample", "line"), P(), P()),
        check_vma=False,
    )
```

profile of v0, /device:TPU:0, one launch (start us, length us, event | category | flops | bytes accessed | tf_op | source)
XLA Modules:
  0.0 207.6 jit_solution(13681144305064519962)
XLA Ops:
  0.6 1.5 broadcast_in_dim.12.refs_4_
  2.1 199.5 %newton_steps.1 = (f32[32,1024]{1,0:T(8,128)}, f32[512,1024]{1,0:T(8,128)}, f32[2,1]{1,0:T(2,128)}) custom-call(bf16[2500,512]{1,0:T(8,128)(2,1)} %bitcast.9, bf16[10000,1024]{1,0:T(8,128)(2,1)} %bitcast.8, bf16[31,10000]{1,0:T(8,128)(2,1)} %refs_2_.1, s32[2,12706]{1,0:T(2,128)} %bitcast.10, f32[1,12706]{1,0:T(1,128)} %broadcast_in_dim.12.refs_4_, ...), custom_call_target="tpu_custom_call" | custom-call | tf_op jit(solution)/shard_map/newton_steps/pallas_call | solution.py:529
  201.6 1.2 fusion
  202.9 1.6 copy.15
  204.4 3.2 %copy.16 = f32[512,1024]{1,0:T(8,128)} copy(f32[512,1024]{1,0:T(8,128)} %get-tuple-element.17) | data formatting | bytes 4194304
where the time goes:
time: 208 us
  Pallas kernels  200 us (96%)
  local copies, waits for them, and re-layouts  7.44 us (4%)
    pallas_call x1, Pallas kernels, newton_steps(): pl.pallas_call(lambda *refs: newton_kernel(samples, ring, chunk, block, g...  200 us
    unnamed x2, local copies, waits for them, and re-layouts  4.73 us

commit v1 on v0

--- a/solution.py
+++ b/solution.py
@@ -73,7 +73,7 @@
     pl.semaphore_wait(barrier, len(partners))
 
 
-def share_steps(samples, ring, features, solved_ref, all_ref, sums_ref, got_ref, mine_ref, far_ref, sends, recvs):
+def share_steps(samples, ring, features, meanwhile, solved_ref, all_ref, sums_ref, got_ref, mine_ref, far_ref, sends, recvs):
     me, place = lax.axis_index("sample"), lax.axis_index("line")
     peers = [lax.rem(me + i, samples) for i in range(1, samples)]
     lines = [lax.rem(place + i, ring) for i in range(1, ring)]
@@ -112,6 +112,7 @@
             )
         )
         far[-1].start()
+    meanwhile()
     total = mine_ref[...]
     for slot in range(ring - 1):
         far[slot].wait_recv()
@@ -146,20 +147,21 @@
 
 def newton_kernel(
     samples, ring, chunk, block, group,
-    wind_ref, ptdf_ref, weights_ref, ends_ref, ratings_ref, monitored_ref, base_ref, cost_ref,
+    wind_ref, ptdf_ref, weights_hbm, ends_hbm, ratings_hbm, monitored_ref, base_ref, cost_ref,
     policy_ref,
     policy_out, flow_out, size_out,
     diff_ref, factors_ref, all_ref, sums_ref, winds, grids, region_mix, stage, table, found, spread, outbox, inbox, mix_inbox,
     packed, weight_mine, policy_mine, cols, solved, step_inbox, mine, far,
     own_sem, stage_sems, send_up, recv_up, send_down, recv_down,
-    send_out, recv_out, send_mix, recv_mix, send_step, recv_step,
+    send_out, recv_out, send_mix, recv_mix, send_rest, recv_rest, send_step, recv_step,
+    rest_out, rest_in, weights_ref, ends_ref, ratings_ref, small_sems,
 ):
     me, mine_s = lax.axis_index("line"), lax.axis_index("sample")
-    regions = weights_ref.shape[0]
+    regions = weights_hbm.shape[0]
     features = regions + 1
     width, scen_here = wind_ref.shape
     total, lines_here = ptdf_ref.shape
-    grid_lines = ends_ref.shape[1]
+    grid_lines = ends_hbm.shape[1]
     share = lines_here // samples
     chunks = scen_here // chunk
     blocks = lines_here // block
@@ -175,28 +177,30 @@
     def rows_of(step):
         return pl.ds(pl.multiple_of(step * chunk, chunk), chunk)
 
-    def transfer(step, hops, side):
+    middle = max(width // 2 // 16 * 16, 16)
+    halves = ((0, middle), (middle, width - middle))
+    ahead = 3
+
+    def slot_of(step, hops, half):
+        return (step * reach + hops - 1) * 2 + half
+
+    def transfer(step, hops, side, half):
         piece = me - side * (hops - 1)
-        slot = step * reach + hops - 1
+        slot = slot_of(step, hops, half)
         rows = rows_of(step)
+        depth = pl.ds(*halves[half])
         first = isinstance(hops, int) and hops == 1
-        source = wind_ref.at[:, rows] if first else winds.at[piece, :, rows]
+        source = wind_ref.at[depth, rows] if first else winds.at[piece, depth, rows]
         sends_, recvs = (send_up, recv_up) if side == 1 else (send_down, recv_down)
         return pltpu.make_async_remote_copy(
             src_ref=source,
-            dst_ref=winds.at[piece, :, rows],
+            dst_ref=winds.at[piece, depth, rows],
             send_sem=sends_.at[slot],
             recv_sem=recvs.at[slot],
             device_id={"line": me + side},
             device_id_type=pl.DeviceIdType.MESH,
         )
 
-    def transfer_first(step):
-        for side in (1, -1):
-            @pl.when(sends(1, side))
-            def _():
-                transfer(step, 1, side).wait_send()
-
     def sends(hops, side):
         if side == 1:
             return jnp.logical_and(me >= hops - 1, me < ring - 1)
@@ -205,15 +209,15 @@
     def receives(hops, side):
         return me >= hops if side == 1 else me < ring - hops
 
-    def launch(step, hops):
+    def launch(step, hops, half):
         for side in (1, -1):
             @pl.when(sends(hops, side))
             def _():
-                transfer(step, hops, side).start()
-
-    def arrival(step, hops, side):
-        slot = step * reach + hops - 1
-        here = winds.at[me - side * hops, :, rows_of(step)]
+                transfer(step, hops, side, half).start()
+
+    def arrival(step, hops, side, half):
+        slot = slot_of(step, hops, half)
+        here = winds.at[me - side * hops, pl.ds(*halves[half]), rows_of(step)]
         pltpu.make_async_remote_copy(
             src_ref=here,
             dst_ref=here,
@@ -223,12 +227,20 @@
             device_id_type=pl.DeviceIdType.MESH,
         ).wait_recv()
 
-    launch(0, 1)
-    if chunks > 1:
-        launch(1, 1)
+    for step in range(min(chunks, ahead)):
+        for half in (0, 1):
+            launch(step, 1, half)
     own = pltpu.make_async_copy(wind_ref, winds.at[me], own_sem)
     own.start()
 
+    small = [
+        pltpu.make_async_copy(source, target, small_sems.at[index])
+        for index, (source, target) in enumerate(
+            [(weights_hbm, weights_ref), (ends_hbm, ends_ref), (ratings_hbm, ratings_ref)]
+        )
+    ]
+    for copy in small:
+        copy.start()
     stage_rows, starts = split_rows(width, total, ring)
 
     def staged(piece, index):
@@ -242,6 +254,8 @@
         )
 
     region_mix[...] = jnp.zeros_like(region_mix)
+    for copy in small:
+        copy.wait()
     for piece in range(ring):
         region_mix[piece, :regions, :] = weights_ref[:, width * piece : width * (piece + 1)]
         skip = width * piece - starts[piece]
@@ -260,7 +274,7 @@
         lax.fori_loop(0, blocks, place, 0)
 
     ends = ends_ref[...]
-    rating_all = ratings_ref[...]
+    rating_all = ratings_ref[...].reshape(1, grid_lines)
     first = rating_all.astype(bf16).astype(f32)
     second = (rating_all - first).astype(bf16).astype(f32)
     third = rating_all - first - second
@@ -310,32 +324,39 @@
 
     forward = (((1,), (0,)), ((), ()))
 
-    def add_piece(step, piece):
+    def add_piece(step, piece, half):
         rows = rows_of(step)
-        wind = winds[piece, :, rows]
+        low, deep = halves[half]
+        depth = pl.ds(low, deep)
+        wind = winds[piece, depth, rows]
         turned = wind.T
-        buses = (
-            lax.broadcasted_iota(jnp.int32, (width, block), 0) + piece * width
-        ).astype(f32)
+        groups = [(cut, min(256, deep - cut)) for cut in range(0, deep, 256)]
+        yes, no = bf16(1), bf16(0)
 
         def one(index, carry):
             lines = pl.ds(pl.multiple_of(index * block, block), block)
-            pick = jnp.where(buses == found[1:2, lines], 1.0, 0.0) - jnp.where(
-                buses == found[0:1, lines], 1.0, 0.0
+            local = found[0:2, lines] - (piece * width + low).astype(f32)
+            picks = []
+            for cut, size in groups:
+                inside = local - float(cut)
+                inside = jnp.where((inside >= 0) & (inside < size), inside, -1.0).astype(bf16)
+                here = lax.broadcasted_iota(jnp.int32, (size, block), 0).astype(f32).astype(bf16)
+                picks.append(
+                    jnp.where(here == inside[1:2], yes, no)
+                    - jnp.where(here == inside[0:1], yes, no)
+                )
+            flow_out[rows, lines] += lax.dot_general(
+                turned, grids[piece, depth, lines], forward, preferred_element_type=f32
             )
-            grid = lax.dot_general(
-                turned, grids[piece, :, lines], forward, preferred_element_type=f32
+            diff_ref[rows, lines] += lax.dot_general(
+                turned, jnp.concatenate(picks, axis=0), forward, preferred_element_type=f32
             )
-            diff = lax.dot_general(
-                turned, pick.astype(bf16), forward, preferred_element_type=f32
-            )
-            flow_out[rows, lines] += grid
-            diff_ref[rows, lines] += diff
             return carry
 
         lax.fori_loop(0, blocks, one, 0)
-        mix = lax.dot_general(region_mix[piece], wind, forward, preferred_element_type=f32)
-        factors_ref[:, rows] += mix
+        factors_ref[:, rows] += lax.dot_general(
+            region_mix[piece, :, depth], wind, forward, preferred_element_type=f32
+        )
 
     def finish(step):
         rows = rows_of(step)
@@ -351,7 +372,13 @@
         flow_out[rows, :] = flow
         for d in range(samples):
             cut = slice(d * share, (d + 1) * share)
-            outbox[d, step, 0] = flow[:, cut].astype(bf16)
+            coarse = flow[:, cut].astype(bf16)
+            outbox[d, step, 0] = coarse
+            if chunks > 1:
+                @pl.when(step < chunks - 1)
+                def _():
+                    rest_out[d, step] = (flow[:, cut] - coarse.astype(f32)).astype(bf16)
+
             outbox[d, step, 1] = diff[:, cut].astype(bf16)
 
     def parcel(step, slot, peer, source):
@@ -374,13 +401,31 @@
             ),
         )
 
+    def remainder(step, slot, peer, source):
+        spot = step * (samples - 1) + slot
+        return pltpu.make_async_remote_copy(
+            src_ref=rest_out.at[peer, step],
+            dst_ref=rest_in.at[source, step],
+            send_sem=send_rest.at[spot],
+            recv_sem=recv_rest.at[spot],
+            device_id={"sample": peer},
+            device_id_type=pl.DeviceIdType.MESH,
+        )
+
     def deliver(step):
         for slot, peer in enumerate(peers):
             for copy in parcel(step, slot, peer, mine_s):
                 copy.start()
 
-    def collect(step):
+        @pl.when(step < chunks - 1)
+        def _():
+            for slot, peer in enumerate(peers):
+                remainder(step, slot, peer, mine_s).start()
+
+    def collect(step, last):
         inbox[mine_s, step] = outbox[mine_s, step]
+        if not last:
+            rest_in[mine_s, step] = rest_out[mine_s, step]
         rating = spread[mine_s, features + 1 : features + 2, :]
 
         def one(turn, carry):
@@ -390,8 +435,12 @@
             def _():
                 for copy in parcel(step, turn - 1, source, source):
                     copy.wait_recv()
+                if not last:
+                    remainder(step, turn - 1, source, source).wait_recv()
 
             flow = inbox[source, step, 0].astype(f32)
+            if not last:
+                flow = flow + rest_in[source, step].astype(f32)
             diff = inbox[source, step, 1].astype(f32)
             factors = mix_inbox[source, step]
             doubled = jnp.concatenate(
@@ -424,48 +473,71 @@
     diff_ref[...] = jnp.zeros_like(diff_ref)
     factors_ref[...] = jnp.zeros_like(factors_ref)
 
-    def advance(step, carry):
-        @pl.when(step + 2 < chunks)
+    def advance(tick, carry):
+        @pl.when(tick + ahead < chunks)
         def _():
-            launch(step + 2, 1)
+            for half in (0, 1):
+                launch(tick + ahead, 1, half)
 
         def visit(turn, inner):
             hops = (turn + 1) // 2
-
-            @pl.when(lax.rem(turn, 2) == 1)
+            step = tick - jnp.maximum(hops - 1, 0)
+            opening = lax.rem(turn, 2) == 1
+            piece = me + hops * (1 - 2 * lax.rem(turn, 2))
+
+            @pl.when(jnp.logical_and(step >= 0, step < chunks))
             def _():
-                for side in (1, -1):
-                    @pl.when(receives(hops, side))
+                for half in (0, 1):
+                    @pl.when(opening)
                     def _():
-                        arrival(step, hops, side)
-
-                @pl.when(hops < reach)
-                def _():
-                    launch(step, hops + 1)
-
-            piece = me + hops * (1 - 2 * lax.rem(turn, 2))
-
-            @pl.when(jnp.logical_and(piece >= 0, piece < ring))
-            def _():
-                add_piece(step, piece)
+                        for side in (1, -1):
+                            @pl.when(receives(hops, side))
+                            def _():
+                                arrival(step, hops, side, half)
+
+                        @pl.when(hops < reach)
+                        def _():
+                            launch(step, hops + 1, half)
+
+                    @pl.when(jnp.logical_and(piece >= 0, piece < ring))
+                    def _():
+                        add_piece(step, piece, half)
 
             return inner
 
         lax.fori_loop(0, 2 * ring - 1, visit, 0)
-        finish(step)
-        deliver(step)
-
-        @pl.when(step > 0)
+        done = tick - (reach - 1)
+
+        @pl.when(done >= 0)
         def _():
-            collect(step - 1)
+            finish(done)
+            deliver(done)
+
+        @pl.when(done > 0)
+        def _():
+            collect(done - 1, False)
 
         return carry
 
-    lax.fori_loop(0, chunks, advance, 0)
-    collect(chunks - 1)
+    lax.fori_loop(0, chunks + reach - 1, advance, 0)
+    collect(chunks - 1, True)
     solve_lines(regions, packed, weight_mine, policy_mine, solved, cols)
+    def full_step():
+        return jnp.concatenate([all_ref[d] for d in range(samples)], axis=1)
+
+    def shifts():
+        steps = full_step()
+
+        def one(step, carry):
+            rows = rows_of(step)
+            turned = factors_ref[:, rows].T
+            diff_ref[rows, :] = dot3(turned, steps) + steps[regions:, :] * diff_ref[rows, :]
+            return carry
+
+        lax.fori_loop(0, chunks, one, 0)
+
     share_steps(
-        samples, ring, features, solved, all_ref, sums_ref, step_inbox, mine, far,
+        samples, ring, features, shifts, solved, all_ref, sums_ref, step_inbox, mine, far,
         send_step, recv_step,
     )
     sizes = jnp.sqrt(jnp.sum(sums_ref[...], axis=1, keepdims=True))
@@ -473,30 +545,34 @@
     scale = 1.0 / (
         1.0 + sizes[:1] / ((barrier_weight * features * lines_here * ring) ** 0.5)
     )
-    scaled = scale * jnp.concatenate([all_ref[d] for d in range(samples)], axis=1)
-    policy_out[...] = policy_ref[...] + scaled
-
-    def update(step, carry):
-        rows = rows_of(step)
-        turned = factors_ref[:, rows].T
-        flow_out[rows, :] += dot3(turned, scaled) + scaled[regions:, :] * diff_ref[rows, :]
-        return carry
-
-    lax.fori_loop(0, chunks, update, 0)
+    policy_out[...] = policy_ref[...] + scale * full_step()
+    flow_out[...] += scale * diff_ref[...]
 
     def drain(step, carry):
         def line_drain(hops, inner):
             for side in (1, -1):
                 @pl.when(sends(hops, side))
                 def _():
-                    transfer(step, hops, side).wait_send()
+                    for half in (0, 1):
+                        transfer(step, hops, side, half).wait_send()
             return inner
 
-        transfer_first(step)
+        for side in (1, -1):
+            @pl.when(sends(1, side))
+            def _():
+                for half in (0, 1):
+                    transfer(step, 1, side, half).wait_send()
+
         lax.fori_loop(2, ring, line_drain, 0)
         for slot, peer in enumerate(peers):
             for copy in parcel(step, slot, peer, mine_s):
                 copy.wait_send()
+
+        @pl.when(step < chunks - 1)
+        def _():
+            for slot, peer in enumerate(peers):
+                remainder(step, slot, peer, mine_s).wait_send()
+
         return carry
 
     lax.fori_loop(0, chunks, drain, 0)
@@ -519,7 +595,7 @@
     table_cols = (incidence.shape[0] + group - 1) // group * group
     stage_rows, _ = split_rows(width, total, ring)
     packed_rows = (features // 2 + 2) * features
-    hops = chunks * (ring - 1)
+    hops = 2 * chunks * (ring - 1)
     parcels = chunks * (samples - 1)
     copies = samples + ring - 2
     vmem = pl.BlockSpec(memory_space=pltpu.VMEM)
@@ -533,7 +609,7 @@
             jax.ShapeDtypeStruct((scen_here, lines_here), f32),
             jax.ShapeDtypeStruct((2, 1), f32),
         ),
-        in_specs=[anywhere, anywhere] + [vmem] * 7,
+        in_specs=[anywhere] * 5 + [vmem] * 4,
         out_specs=(vmem,) * 3,
         scratch_shapes=[
             pltpu.VMEM((scen_here, lines_here), f32),
@@ -568,22 +644,59 @@
             dma((parcels,)),
             dma((parcels,)),
             dma((parcels,)),
+            dma((parcels,)),
+            dma((parcels,)),
             dma((copies,)),
             dma((copies,)),
+            pltpu.VMEM((samples, chunks, chunk, share), bf16),
+            pltpu.VMEM((samples, chunks, chunk, share), bf16),
+            pltpu.VMEM(region_weights.shape, bf16),
+            pltpu.VMEM(incidence.shape[::-1], jnp.int32),
+            pltpu.VMEM(ratings.shape, f32),
+            dma((3,)),
         ],
         compiler_params=pltpu.CompilerParams(
             collective_id=0, has_side_effects=True, vmem_limit_bytes=67000000
         ),
         name="newton_steps",
     )(
-        wind_dev.T, ptdf.T, region_weights, incidence.T, ratings[None, :], monitored[None, :],
+        wind_dev.T, ptdf.T, region_weights, incidence.T, ratings, monitored[None, :],
         base_flow[None, :], line_cost[None, :], policy,
     )
 
 
+def hand_over(new_policy, new_flows, sizes):
+    scen_here, lines_here = new_flows.shape
+    rows = scen_here // 4
+
+    def pass_on(policy_ref, flow_ref, sizes_ref, policy_out, flow_out, *size_outs):
+        policy_out[...] = policy_ref[...]
+        flow_out[...] = flow_ref[...]
+        for row, size_out in enumerate(size_outs):
+            size_out[...] = sizes_ref[row : row + 1, :]
+
+    def whole(shape):
+        return pl.BlockSpec(shape, lambda step: (0, 0))
+
+    flow_block = pl.BlockSpec((rows, lines_here), lambda step: (step, 0))
+    return pl.pallas_call(
+        pass_on,
+        grid=(4,),
+        in_specs=[whole(new_policy.shape), flow_block, whole(sizes.shape)],
+        out_specs=(whole(new_policy.shape), flow_block, whole((1, 1)), whole((1, 1))),
+        out_shape=(
+            jax.ShapeDtypeStruct(new_policy.shape, jnp.float32),
+            jax.ShapeDtypeStruct(new_flows.shape, jnp.float32),
+            jax.ShapeDtypeStruct((1, 1), jnp.float32),
+            jax.ShapeDtypeStruct((1, 1), jnp.float32),
+        ),
+        name="hand_over",
+    )(new_policy, new_flows, sizes)
+
+
 def shards(*arrays):
-    new_policy, new_flows, sizes = newton_steps(*arrays)
-    return new_policy, new_flows, sizes[0, 0], sizes[1, 0]
+    new_policy, new_flows, decrement, grad_norm = hand_over(*newton_steps(*arrays))
+    return new_policy, new_flows, decrement.reshape(()), grad_norm.reshape(())
 
 
 def solution(mesh):

time: 208 us -> 202 us (0.971)
  local copies, waits for them, and re-layouts: 7.44 us -> 0 us
    unnamed x2 -> x0, local copies, waits for them, and re-layouts: 4.73 us -> none
    pallas_call x0 -> x1, Pallas kernels: none -> 3.88 us  [hand_over(): pl.pallas_call(pass_on, grid=(4,), in_specs=[whole(new_policy.shape), flo...]
    pallas_call x1, Pallas kernels: 200 us -> 197 us  [newton_steps(): pl.pallas_call(lambda *refs: newton_kernel(samples, ring, chunk, block, g...]
where the time goes in v1:
time: 202 us
  Pallas kernels  201 us (100%)
    pallas_call x1, Pallas kernels, newton_steps(): pl.pallas_call(lambda *refs: newton_kernel(samples, ring, chunk, block, g...  197 us

profile of v1, /device:TPU:0, one launch (start us, length us, event | category | flops | bytes accessed | tf_op | source)
XLA Modules:
  0.0 201.8 jit_solution(13914153325735944190)
XLA Ops:
  0.6 197.2 %newton_steps.1 = (f32[32,1024]{1,0:T(8,128)}, f32[512,1024]{1,0:T(8,128)}, f32[2,1]{1,0:T(2,128)}) custom-call(bf16[2500,512]{1,0:T(8,128)(2,1)} %bitcast.9, bf16[10000,1024]{1,0:T(8,128)(2,1)} %bitcast.8, bf16[31,10000]{1,0:T(8,128)(2,1)} %refs_2_.1, s32[2,12706]{1,0:T(2,128)} %bitcast.10, f32[12706]{0:T(1024)} %refs_4_.1, s32[1,1024]{1,0:T(1,128)} %bitcast.11, ...), custom_call_target="tpu_custom_call" | custom-call | tf_op jit(solution)/shard_map/newton_steps/pallas_call | solution.py:605
  197.9 3.9 %hand_over.1 = (f32[32,1024]{1,0:T(8,128)}, f32[512,1024]{1,0:T(8,128)}, f32[1,1]{1,0:T(1,128)}, f32[1,1]{1,0:T(1,128)}) custom-call(f32[32,1024]{1,0:T(8,128)} %get-tuple-element.11.policy_ref, f32[512,1024]{1,0:T(8,128)} %get-tuple-element.12.flow_ref, f32[2,1]{1,0:T(2,128)} %get-tuple-element.13.sizes_ref), custom_call_target="tpu_custom_call" | custom-call | tf_op jit(solution)/shard_map/hand_over/pallas_call | solution.py:682

commit v2 on v1

--- a/solution.py
+++ b/solution.py
@@ -147,14 +147,15 @@
 
 def newton_kernel(
     samples, ring, chunk, block, group,
-    wind_ref, ptdf_ref, weights_hbm, ends_hbm, ratings_hbm, monitored_ref, base_ref, cost_ref,
-    policy_ref,
-    policy_out, flow_out, size_out,
+    wind_ref, ptdf_ref, weights_hbm, ends_hbm, ratings_hbm, monitored_hbm, base_hbm, cost_hbm,
+    policy_hbm,
+    policy_out, flow_out, decrement_out, norm_out,
     diff_ref, factors_ref, all_ref, sums_ref, winds, grids, region_mix, stage, table, found, spread, outbox, inbox, mix_inbox,
     packed, weight_mine, policy_mine, cols, solved, step_inbox, mine, far,
     own_sem, stage_sems, send_up, recv_up, send_down, recv_down,
     send_out, recv_out, send_mix, recv_mix, send_rest, recv_rest, send_step, recv_step,
-    rest_out, rest_in, weights_ref, ends_ref, ratings_ref, small_sems,
+    rest_out, rest_in, weights_ref, ends_ref, ratings_ref, monitored_ref, base_ref, cost_ref,
+    policy_ref, small_sems,
 ):
     me, mine_s = lax.axis_index("line"), lax.axis_index("sample")
     regions = weights_hbm.shape[0]
@@ -236,7 +237,15 @@
     small = [
         pltpu.make_async_copy(source, target, small_sems.at[index])
         for index, (source, target) in enumerate(
-            [(weights_hbm, weights_ref), (ends_hbm, ends_ref), (ratings_hbm, ratings_ref)]
+            [
+                (weights_hbm, weights_ref),
+                (ends_hbm, ends_ref),
+                (ratings_hbm, ratings_ref),
+                (monitored_hbm, monitored_ref),
+                (base_hbm, base_ref),
+                (cost_hbm, cost_ref),
+                (policy_hbm, policy_ref),
+            ]
         )
     ]
     for copy in small:
@@ -428,21 +437,30 @@
             rest_in[mine_s, step] = rest_out[mine_s, step]
         rating = spread[mine_s, features + 1 : features + 2, :]
 
+        batch = 2 if samples % 2 == 0 else 1
+
         def one(turn, carry):
-            source = lax.rem(mine_s + samples - turn, samples)
-
-            @pl.when(turn > 0)
-            def _():
-                for copy in parcel(step, turn - 1, source, source):
-                    copy.wait_recv()
+            flows, diffs, mixes = [], [], []
+            for inner in range(batch):
+                order = turn * batch + inner
+                source = lax.rem(mine_s + samples - order, samples)
+
+                @pl.when(order > 0)
+                def _():
+                    for copy in parcel(step, order - 1, source, source):
+                        copy.wait_recv()
+                    if not last:
+                        remainder(step, order - 1, source, source).wait_recv()
+
+                flow = inbox[source, step, 0].astype(f32)
                 if not last:
-                    remainder(step, turn - 1, source, source).wait_recv()
-
-            flow = inbox[source, step, 0].astype(f32)
-            if not last:
-                flow = flow + rest_in[source, step].astype(f32)
-            diff = inbox[source, step, 1].astype(f32)
-            factors = mix_inbox[source, step]
+                    flow = flow + rest_in[source, step].astype(f32)
+                flows.append(flow)
+                diffs.append(inbox[source, step, 1].astype(f32))
+                mixes.append(mix_inbox[source, step])
+            flow = jnp.concatenate(flows, axis=0)
+            diff = jnp.concatenate(diffs, axis=0)
+            factors = jnp.concatenate(mixes, axis=1)
             doubled = jnp.concatenate(
                 [factors[:regions], factors[:regions], factors[regions:]], axis=0
             )
@@ -455,19 +473,17 @@
             curve = (prob_up * (1.0 - prob_up) + prob_down * (1.0 - prob_down)) / smoothing
             weighted = curve * diff
             top = bands * features
+            low = top + features
             packed[:top, :] += dot3(pairs, curve)
             packed[top : top + regions, :] += dot3(factors, weighted)[:regions]
-            packed[top + regions : top + features, :] += jnp.sum(
-                weighted * diff, axis=0, keepdims=True
-            )
-            low = top + features
+            packed[top + regions : low, :] += jnp.sum(weighted * diff, axis=0, keepdims=True)
             packed[low : low + regions, :] += dot3(factors, slope)[:regions]
             packed[low + regions : low + features, :] += jnp.sum(
                 slope * diff, axis=0, keepdims=True
             )
             return carry
 
-        lax.fori_loop(0, samples, one, 0)
+        lax.fori_loop(0, samples // batch, one, 0)
 
     flow_out[...] = jnp.zeros_like(flow_out)
     diff_ref[...] = jnp.zeros_like(diff_ref)
@@ -541,7 +557,8 @@
         send_step, recv_step,
     )
     sizes = jnp.sqrt(jnp.sum(sums_ref[...], axis=1, keepdims=True))
-    size_out[...] = sizes[:2]
+    decrement_out[...] = sizes[:1]
+    norm_out[...] = sizes[1:2]
     scale = 1.0 / (
         1.0 + sizes[:1] / ((barrier_weight * features * lines_here * ring) ** 0.5)
     )
@@ -599,18 +616,19 @@
     parcels = chunks * (samples - 1)
     copies = samples + ring - 2
     vmem = pl.BlockSpec(memory_space=pltpu.VMEM)
-    anywhere = pl.BlockSpec(memory_space=pl.ANY)
+    far_off = pl.BlockSpec(memory_space=pltpu.HBM)
     f32, bf16 = jnp.float32, jnp.bfloat16
     dma = pltpu.SemaphoreType.DMA
     return pl.pallas_call(
         lambda *refs: newton_kernel(samples, ring, chunk, block, group, *refs),
         out_shape=(
-            jax.ShapeDtypeStruct((features, lines_here), f32),
-            jax.ShapeDtypeStruct((scen_here, lines_here), f32),
-            jax.ShapeDtypeStruct((2, 1), f32),
+            pltpu.VMEM((features, lines_here), f32),
+            pltpu.VMEM((scen_here, lines_here), f32),
+            pltpu.VMEM((1, 1), f32),
+            pltpu.VMEM((1, 1), f32),
         ),
-        in_specs=[anywhere] * 5 + [vmem] * 4,
-        out_specs=(vmem,) * 3,
+        in_specs=[far_off] * 9,
+        out_specs=(vmem,) * 4,
         scratch_shapes=[
             pltpu.VMEM((scen_here, lines_here), f32),
             pltpu.VMEM((features, scen_here), f32),
@@ -653,10 +671,14 @@
             pltpu.VMEM(region_weights.shape, bf16),
             pltpu.VMEM(incidence.shape[::-1], jnp.int32),
             pltpu.VMEM(ratings.shape, f32),
-            dma((3,)),
+            pltpu.VMEM((1, lines_here), jnp.int32),
+            pltpu.VMEM((1, lines_here), f32),
+            pltpu.VMEM((1, lines_here), f32),
+            pltpu.VMEM(policy.shape, f32),
+            dma((7,)),
         ],
         compiler_params=pltpu.CompilerParams(
-            collective_id=0, has_side_effects=True, vmem_limit_bytes=67000000
+            collective_id=0, has_side_effects=True, vmem_limit_bytes=60000000
         ),
         name="newton_steps",
     )(
@@ -665,37 +687,8 @@
     )
 
 
-def hand_over(new_policy, new_flows, sizes):
-    scen_here, lines_here = new_flows.shape
-    rows = scen_here // 4
-
-    def pass_on(policy_ref, flow_ref, sizes_ref, policy_out, flow_out, *size_outs):
-        policy_out[...] = policy_ref[...]
-        flow_out[...] = flow_ref[...]
-        for row, size_out in enumerate(size_outs):
-            size_out[...] = sizes_ref[row : row + 1, :]
-
-    def whole(shape):
-        return pl.BlockSpec(shape, lambda step: (0, 0))
-
-    flow_block = pl.BlockSpec((rows, lines_here), lambda step: (step, 0))
-    return pl.pallas_call(
-        pass_on,
-        grid=(4,),
-        in_specs=[whole(new_policy.shape), flow_block, whole(sizes.shape)],
-        out_specs=(whole(new_policy.shape), flow_block, whole((1, 1)), whole((1, 1))),
-        out_shape=(
-            jax.ShapeDtypeStruct(new_policy.shape, jnp.float32),
-            jax.ShapeDtypeStruct(new_flows.shape, jnp.float32),
-            jax.ShapeDtypeStruct((1, 1), jnp.float32),
-            jax.ShapeDtypeStruct((1, 1), jnp.float32),
-        ),
-        name="hand_over",
-    )(new_policy, new_flows, sizes)
-
-
 def shards(*arrays):
-    new_policy, new_flows, decrement, grad_norm = hand_over(*newton_steps(*arrays))
+    new_policy, new_flows, decrement, grad_norm = newton_steps(*arrays)
     return new_policy, new_flows, decrement.reshape(()), grad_norm.reshape(())
 
 

time: 202 us -> 200 us (0.990)
  Pallas kernels: 201 us -> 195 us
  between operations: 0.64 us -> 2.97 us
    pallas_call x1 -> x0, Pallas kernels: 3.88 us -> none  [hand_over(): pl.pallas_call(pass_on, grid=(4,), in_specs=[whole(new_policy.shape), flo...]
    pallas_call x1, Pallas kernels: 197 us -> 195 us  [newton_steps(): pl.pallas_call(lambda *refs: newton_kernel(samples, ring, chunk, block, g...]
where the time goes in v2:
time: 200 us
  Pallas kernels  195 us (98%)
  between operations  2.97 us (1%)
    pallas_call x1, Pallas kernels, newton_steps(): pl.pallas_call(lambda *refs: newton_kernel(samples, ring, chunk, block, g...  195 us

profile of v2, /device:TPU:0, one launch (start us, length us, event | category | flops | bytes accessed | tf_op | source)
XLA Modules:
  0.0 199.6 jit_solution(11845863552139687257)
XLA Ops:
  0.6 194.7 %newton_steps.1 = (f32[32,1024]{1,0:T(8,128)S(1)}, f32[512,1024]{1,0:T(8,128)S(1)}, f32[1,1]{1,0:T(1,128)S(1)}, f32[1,1]{1,0:T(1,128)S(1)}) custom-call(bf16[2500,512]{1,0:T(8,128)(2,1)} %bitcast.9, bf16[10000,1024]{1,0:T(8,128)(2,1)} %bitcast.8, bf16[31,10000]{1,0:T(8,128)(2,1)} %refs_2_.1, s32[2,12706]{1,0:T(2,128)} %bitcast.10, f32[12706]{0:T(1024)} %refs_4_.1, ...), custom_call_target="tpu_custom_call" | custom-call | tf_op jit(solution)/shard_map/newton_steps/pallas_call | solution.py:622
  195.4 0.7 copy.17
  196.1 1.3 copy.18

commit v3 on v2

--- a/solution.py
+++ b/solution.py
@@ -367,29 +367,6 @@
             region_mix[piece, :, depth], wind, forward, preferred_element_type=f32
         )
 
-    def finish(step):
-        rows = rows_of(step)
-        turned = factors_ref[:, rows].T
-        mix_inbox[mine_s, step] = factors_ref[:, rows]
-        diff = diff_ref[rows, :]
-        flow = (
-            flow_out[rows, :]
-            + base_ref[...]
-            + dot3(turned, policy_ref[...])
-            + policy_ref[regions:, :] * diff
-        )
-        flow_out[rows, :] = flow
-        for d in range(samples):
-            cut = slice(d * share, (d + 1) * share)
-            coarse = flow[:, cut].astype(bf16)
-            outbox[d, step, 0] = coarse
-            if chunks > 1:
-                @pl.when(step < chunks - 1)
-                def _():
-                    rest_out[d, step] = (flow[:, cut] - coarse.astype(f32)).astype(bf16)
-
-            outbox[d, step, 1] = diff[:, cut].astype(bf16)
-
     def parcel(step, slot, peer, source):
         spot = step * (samples - 1) + slot
         common = dict(device_id={"sample": peer}, device_id_type=pl.DeviceIdType.MESH)
@@ -421,15 +398,49 @@
             device_id_type=pl.DeviceIdType.MESH,
         )
 
-    def deliver(step):
+    owners = block // share
+
+    def finish(step):
+        rows = rows_of(step)
+        turned = factors_ref[:, rows].T
+        mix_inbox[mine_s, step] = factors_ref[:, rows]
         for slot, peer in enumerate(peers):
-            for copy in parcel(step, slot, peer, mine_s):
-                copy.start()
-
-        @pl.when(step < chunks - 1)
-        def _():
-            for slot, peer in enumerate(peers):
-                remainder(step, slot, peer, mine_s).start()
+            parcel(step, slot, peer, mine_s)[1].start()
+
+        def one(turn, carry):
+            index = lax.rem(mine_s // owners + 1 + turn, blocks)
+            lines = pl.ds(pl.multiple_of(index * block, block), block)
+            diff = diff_ref[rows, lines]
+            flow = (
+                flow_out[rows, lines]
+                + base_ref[:, lines]
+                + dot3(turned, policy_ref[:, lines])
+                + policy_ref[regions:, lines] * diff
+            )
+            flow_out[rows, lines] = flow
+            for inner in range(owners):
+                cut = slice(inner * share, (inner + 1) * share)
+                peer = index * owners + inner
+                slot = lax.rem(peer - mine_s - 1 + samples, samples)
+                coarse = flow[:, cut].astype(bf16)
+                outbox[peer, step, 0] = coarse
+                outbox[peer, step, 1] = diff[:, cut].astype(bf16)
+                if chunks > 1:
+                    @pl.when(step < chunks - 1)
+                    def _():
+                        rest_out[peer, step] = (flow[:, cut] - coarse.astype(f32)).astype(bf16)
+
+                @pl.when(peer != mine_s)
+                def _():
+                    parcel(step, slot, peer, mine_s)[0].start()
+
+                    @pl.when(step < chunks - 1)
+                    def _():
+                        remainder(step, slot, peer, mine_s).start()
+
+            return carry
+
+        lax.fori_loop(0, blocks, one, 0)
 
     def collect(step, last):
         inbox[mine_s, step] = outbox[mine_s, step]
@@ -527,7 +538,6 @@
         @pl.when(done >= 0)
         def _():
             finish(done)
-            deliver(done)
 
         @pl.when(done > 0)
         def _():

time: 200 us -> 200 us (level)
  no operation moved by 1% of the time
where the time goes in v3:
time: 200 us; the launch traced here: 199 us
  Pallas kernels  194 us (97%)
  between operations  2.97 us (1%)
    pallas_call x1, Pallas kernels, newton_steps(): pl.pallas_call(lambda *refs: newton_kernel(samples, ring, chunk, block, g...  194 us

profile of v3, /device:TPU:0, one launch (start us, length us, event | category | flops | bytes accessed | tf_op | source)
XLA Modules:
  0.0 199.4 jit_solution(10687905841787567625)
XLA Ops:
  0.6 194.4 %newton_steps.1 = (f32[32,1024]{1,0:T(8,128)S(1)}, f32[512,1024]{1,0:T(8,128)S(1)}, f32[1,1]{1,0:T(1,128)S(1)}, f32[1,1]{1,0:T(1,128)S(1)}) custom-call(bf16[2500,512]{1,0:T(8,128)(2,1)} %bitcast.9, bf16[10000,1024]{1,0:T(8,128)(2,1)} %bitcast.8, bf16[31,10000]{1,0:T(8,128)(2,1)} %refs_2_.1, s32[2,12706]{1,0:T(2,128)} %bitcast.10, f32[12706]{0:T(1024)} %refs_4_.1, ...), custom_call_target="tpu_custom_call" | custom-call | tf_op jit(solution)/shard_map/newton_steps/pallas_call | solution.py:632
  195.1 0.7 copy.17
  195.8 1.3 copy.18
